TPU v7x, 32 devices: a whole 2x2x4 slice. The times are simulated.
32 devices in a mesh: row: 8 (over z, core), col: 4 (over y, x).
Axes of the slice: x: 2, y: 2, z: 4, core: 2. Of those that a mesh axis runs over, the one named last changes fastest.
Arguments:
- vectors: bfloat16 [2, 4, 16384], P(None, 'col', 'row'), may hold values from -6 to 6
- lr_left: bfloat16 [8, 4, 32, 8, 2048], P('row', 'col'), may hold values from -0.75 to 0.75
- lr_right: bfloat16 [8, 4, 32, 8, 2048], P('row', 'col'), may hold values from -0.125 to 0.125
- tile_rank: int32 [8, 4, 32], P('row', 'col'), may hold values from 0 to 8, as said below
- leaf_values: bfloat16 [8, 4, 8, 512, 512], P('row', 'col'), may hold values from -0.25 to 0.25
- leaf_places: int32 [8, 4, 8, 2], P('row', 'col'), may hold values from 0 to 31, as said below
- cluster_perm: int32 [8, 8192], P('row'), may hold values from 0 to 65535, as said below
- kappa: float32 [32, 16, 128], P('row', 'col'), may hold values from 0.25 to 4
Outputs:
- prior_action: float32 [2, 32, 16, 128], P(None, 'row', 'col')
Inputs may be any that keep to these rules, and one draw needn't show every extreme that they name: `tile_rank`: 0 exactly on the tiles that contain a leaf, 1 to 8 on the others. `leaf_places`: the 8 leaves of a block are distinct; entry 0 indexes rows and entry 1 column of the block in units of 512. `cluster_perm`: a permutation of all brick indices; within each aligned block of 2048 entries, every value of entry // 2048 occurs exactly 128 times or not at all.
All inputs are finite; a program needn't handle non-finite values.
Results may differ from a plain program's by a relative error of at most 0.0023.
Values may be sent and summed in bfloat16 or wider, within the bound.
A program may use at most 64 MiB of HBM per device.

v0:
```python
import jax
import jax.numpy as jnp
from jax import lax
from jax.sharding import PartitionSpec as P

NVEC = 2
CX = 4
CY = 4
NZ = 128
TILE_ROWS = 4
TILE_COLS = 8
KMAX = 8
LEAF = 512


def extended(cells, sides, width):
    for axis, dim in sides:
        count = lax.axis_size(axis)
        ends = count - 1
        head = lax.slice_in_dim(cells, 0, width, axis=dim)
        tail = lax.slice_in_dim(cells, cells.shape[dim] - width, cells.shape[dim], axis=dim)
        cells = jnp.concatenate(
            [
                lax.ppermute(tail, axis, [(i, (i + 1) % count) for i in range(ends)]),
                cells,
                lax.ppermute(head, axis, [((i + 1) % count, i) for i in range(ends)]),
            ],
            axis=dim,
        )
    return cells


def prior_step(padded, stiffness):
    center = padded[:, 1:-1, 1:-1, :]
    flat_pad = jnp.pad(center, ((0, 0), (0, 0), (0, 0), (1, 1)))
    beside = padded[:, 2:, 1:-1, :] + padded[:, :-2, 1:-1, :]
    beside = beside + padded[:, 1:-1, 2:, :] + padded[:, 1:-1, :-2, :]
    beside = beside + flat_pad[..., 2:] + flat_pad[..., :-2]
    return ((6.0 + stiffness) * center - beside) * 0.125


def route(values, targets, groups, points, capacity, devices):
    target_dev = targets // points
    places = targets % points
    grouped = target_dev.reshape(groups, points)
    one_hot = (grouped[:, :, None] == jnp.arange(devices)[None, None, :]).astype(jnp.int32)
    running = jnp.cumsum(one_hot, axis=1)
    within = jnp.sum(running * one_hot, axis=2) - 1
    slot_index = jnp.arange(groups)[:, None] * capacity + within
    buffer_at = (grouped * (groups * capacity) + slot_index).reshape(-1)
    buffer_len = devices * groups * capacity
    send_values = jnp.zeros((values.shape[0], buffer_len), jnp.float32).at[:, buffer_at].set(values)
    send_places = jnp.full((1, buffer_len), points, jnp.int32).at[0, buffer_at].set(places)
    return (send_values, send_places)


def per_device(
    vectors, lr_left, lr_right, tile_rank, leaf_values, leaf_places, cluster_perm, kappa
):
    gathered = lax.all_gather(vectors, "row", axis=2, tiled=True)
    x_column = gathered[:, 0, :]
    tile_size = lr_left.shape[-1]
    rows_len = tile_size * TILE_ROWS
    x_tiles = x_column.reshape(NVEC, TILE_COLS, tile_size)
    far_right = lr_right[0, 0].reshape(TILE_ROWS, TILE_COLS, KMAX, tile_size)
    projected = jnp.einsum("abkp,vbp->abvk", far_right, x_tiles, preferred_element_type=jnp.float32)
    rank_mask = (
        jnp.arange(KMAX)[None, None, :] < tile_rank[0, 0].reshape(TILE_ROWS, TILE_COLS)[:, :, None]
    ).astype(jnp.float32)
    projected = (projected * rank_mask[:, :, None, :]).astype(jnp.bfloat16)
    far_left = lr_left[0, 0].reshape(TILE_ROWS, TILE_COLS, KMAX, tile_size)
    far_part = jnp.einsum(
        "abkp,abvk->vap", far_left, projected, preferred_element_type=jnp.float32
    ).reshape(NVEC, rows_len)
    leaf_pos = leaf_places[0, 0]
    x_sub = x_column.reshape(NVEC, x_column.shape[1] // LEAF, LEAF)
    picked = jnp.take(x_sub, leaf_pos[:, 1], axis=1)
    near_out = jnp.einsum(
        "lqp,vlp->vlq", leaf_values[0, 0], picked, preferred_element_type=jnp.float32
    )
    selector = (leaf_pos[:, 0][:, None] == jnp.arange(rows_len // LEAF)[None, :]).astype(
        jnp.float32
    )
    near_part = jnp.einsum("vlq,lr->vrq", near_out, selector, precision=lax.Precision.HIGHEST)
    partial_sums = far_part + near_part.reshape(NVEC, rows_len)
    points = vectors.shape[2]
    devices = lax.axis_size("row") * lax.axis_size("col")
    capacity = 2 * points // devices
    summed = lax.psum_scatter(partial_sums, "col", scatter_dimension=1, tiled=True)
    targets = lax.dynamic_slice_in_dim(cluster_perm[0], lax.axis_index("col") * points, points)
    send_values, send_places = route(summed, targets, 1, points, capacity, devices)
    received_values, received_places = (
        lax.all_to_all(send_values, ("row", "col"), split_axis=1, concat_axis=1, tiled=True),
        lax.all_to_all(send_places, ("row", "col"), split_axis=1, concat_axis=1, tiled=True),
    )
    field = (
        jnp.zeros((NVEC, points + 1), jnp.float32).at[:, received_places[0]].add(received_values)
    )
    field = field[:, :points].reshape(NVEC, CX, CY, NZ)
    for repeat in range(4):
        padded = extended(field, (("row", 1), ("col", 2)), 1)
        field = prior_step(padded, kappa)
    return field


def solution(mesh):
    in_specs = (
        P(None, "col", "row"),
        P("row", "col", None, None, None),
        P("row", "col", None, None, None),
        P("row", "col", None),
        P("row", "col", None, None, None),
        P("row", "col", None, None),
        P("row", None),
        P("row", "col", None),
    )
    out_specs = P(None, "row", "col", None)
    return jax.shard_map(
        per_device, mesh=mesh, in_specs=in_specs, out_specs=out_specs, check_vma=False
    )
```

profile of v0, /device:TPU:12, one launch (start us, length us, event | category | flops | bytes accessed | tf_op | source)
XLA Modules:
  0.0 208.1 jit_solution(8211785777179416884)
XLA Ops:
  8.0 14.4 %all_gather.3 = bf16[2,1,16384]{2,0,1:T(2,128)(2,1)S(1)} all-gather(bf16[2,1,2048]{2,0,1:T(2,128)(2,1)} %param.8), channel_id=1, replica_groups=mesh['row'=8,'col'=4] {'row'}, dimensions={2}, use_global_device_ids=true | all-gather | bytes 73728 | tf_op jit(solution)/shard_map/all_gather | solution.py:60
  23.1 3.5 %fusion.2 = f32[2,8,512]{2,0,1:T(2,128)S(1)} fusion(bf16[1,1,8,512,512]{4,3,2,1,0:T(8,128)(2,1)} %param.12, bf16[8,2,512]{2,1,0:T(2,128)(2,1)S(1)} %gather_fusion, pred[8]{0:T(512)(128)(4,1)S(1)} %and_bitcast_fusion), kind=kOutput, calls=%fused_computation.7 | convolution fusion | flops 8396800 | bytes 4243464 | tf_op jit(solution)/shard_map/lqp,vlp->vlq/dot_general | solution.py:78
  28.2 2.8 %fusion.7 = f32[4,2,2048,1]{2,1,3,0:T(2,128)S(1)} fusion(bf16[4,8,8,2048]{3,2,1,0:T(8,128)(2,1)S(1)} %bitcast.79, bf16[2,8,2048,1]{2,0,1,3:T(2,128)(2,1)S(1)} %bitcast.87, bf16[4,8,8,2048]{3,2,1,0:T(8,128)(2,1)S(1)} %bitcast.84, f32[4,8,8]{2,1,0:T(8,128)S(1)} %fusion.42), kind=kOutput, calls=%fused_computation.11 | convolution fusion | flops 4195328 | bytes 2229248 | tf_op jit(solution)/shard_map/abkp,abvk->vap/dot_general | solution.py:72
  31.0 2.7 %copy.53 = f32[2,8192]{0,1:T(8,128)} copy(f32[2,8192]{1,0:T(2,128)S(1)} %add.151) | data formatting | bytes 131072
  34.5 9.1 %reduce-window.6 = s32[1,32,16,128]{3,2,1,0:T(8,128)S(1)} reduce-window(s32[1,32,16,128]{3,2,1,0:T(8,128)S(1)} %bitcast.83, s32[]{:T(128)} %constant.61.clone.1), window={size=1x1x1x128 pad=0_0x0_0x0_0x127_0}, to_apply=%region_0.1 | reduce-window | flops 8323072 | bytes 524292 | tf_op jit(solution)/shard_map/reduce-window
  44.8 8.6 %scatter_custom_fusion.2 = s32[4096]{0:T(1024)} fusion(s32[2048]{0:T(1024)S(1)} %broadcast_select_fusion.2, s32[2048]{0:T(1024)S(1)} %get-tuple-element.29, s32[]{:T(128)} %constant.60.clone.1), kind=kCustom, calls=%fused_computation.107 | custom fusion | bytes 16388
  53.4 5.8 %all-to-all-start = ((s32[1,32,128]{2,0,1:T(1,128)}), s32[1,32,128]{2,0,1:T(1,128)S(1)}, u32[]{:S(2)}, u32[]{:S(2)}) async-start(s32[1,32,128]{2,0,1:T(1,128)} %bitcast.7), calls=%async_computation | async-start | bytes 32768 | tf_op jit(solution)/shard_map/all_to_all | solution.py:94
  59.2 28.3 %reduce-scatter.4.cloned.1.call-done = f32[2048,2]{1,0:T(8,128)} async-done(((f32[8192,2]{1,0:T(8,128)}), f32[2048,2]{1,0:T(8,128)}) %reduce-scatter.4.cloned.1.call-update) | async-done | bytes 16400
  90.5 6.5 %scatter_custom_fusion = f32[2,4096]{0,1:T(8,128)S(1)} fusion(s32[2048]{0:T(1024)S(1)} %bitcast.91, f32[2048,2]{1,0:T(8,128)} %copy.42, f32[]{:T(128)} %constant.59.clone.1), kind=kCustom, calls=%fused_computation.12 | custom fusion | bytes 33280 | tf_op jit(solution)/shard_map/scatter | solution.py:52
  98.1 4.9 %all-to-all-start.1 = ((f32[2,32,128]{2,0,1:T(2,128)}), f32[2,32,128]{2,0,1:T(2,128)S(1)}, u32[]{:S(2)}, u32[]{:S(2)}) async-start(f32[2,32,128]{2,0,1:T(2,128)} %copy.43), calls=%async_computation.1 | async-start | bytes 65536 | tf_op jit(solution)/shard_map/all_to_all | solution.py:93
  103.1 5.1 %all-to-all-done.1 = f32[2,32,128]{2,0,1:T(2,128)S(1)} async-done(((f32[2,32,128]{2,0,1:T(2,128)}), f32[2,32,128]{2,0,1:T(2,128)S(1)}, u32[]{:S(2)}, u32[]{:S(2)}) %all-to-all-start.1) | async-done | bytes 32800 | tf_op jit(solution)/shard_map/all_to_all | solution.py:93
  110.2 26.0 %scatter_custom_fusion.1 = f32[2,2049]{0,1:T(8,128)S(1)} fusion(s32[4096]{0:T(1024)S(1)} %bitcast.96, f32[4096,2]{1,0:T(8,128)} %copy.44, f32[]{:T(128)} %constant.59.clone.1), kind=kCustom, calls=%fused_computation.14 | custom fusion | flops 8192 | bytes 16904 | tf_op jit(solution)/shard_map/scatter-add | solution.py:97
  136.6 3.0 %collective-permute-start = (f32[2,1,4,128]{3,2,1,0:T(4,128)S(1)}, f32[2,1,4,128]{3,2,1,0:T(4,128)S(1)}, u32[]{:S(2)}, u32[]{:S(2)}) collective-permute-start(f32[2,1,4,128]{3,2,1,0:T(4,128)S(1)} %get-tuple-element.26), channel_id=1, source_target_pairs={{4,0},{8,4},{12,8},{16,12},{20,16},{24,20},{28,24},{5,1},{9,5},{13... | collective-permute-start | bytes 12296 | tf_op jit(solution)/shard_map/ppermute | solution.py:26
  141.5 3.0 %collective-permute-done.1 = f32[2,1,4,128]{3,2,1,0:T(4,128)S(1)} collective-permute-done((f32[2,1,4,128]{3,2,1,0:T(4,128)S(1)}, f32[2,1,4,128]{3,2,1,0:T(4,128)S(1)}, u32[]{:S(2)}, u32[]{:S(2)}) %collective-permute-start.1) | collective-permute-done | bytes 4128 | tf_op jit(solution)/shard_map/ppermute | solution.py:24
  144.5 3.4 %collective-permute-start.2 = (f32[2,6,1,128]{3,2,1,0:T(1,128)S(1)}, f32[2,6,1,128]{3,2,1,0:T(1,128)S(1)}, u32[]{:S(2)}, u32[]{:S(2)}) collective-permute-start(f32[2,6,1,128]{3,2,1,0:T(1,128)S(1)} %get-tuple-element.17), channel_id=1, source_target_pairs={{1,0},{2,1},{3,2},{5,4},{6,5},{7,6},{9,8},{10,9},{11,10},{13,12},{... | collective-permute-start | bytes 18440 | tf_op jit(solution)/shard_map/ppermute | solution.py:26
  150.4 3.9 %collective-permute-done.3 = f32[2,6,1,128]{3,2,1,0:T(1,128)S(1)} collective-permute-done((f32[2,6,1,128]{3,2,1,0:T(1,128)S(1)}, f32[2,6,1,128]{3,2,1,0:T(1,128)S(1)}, u32[]{:S(2)}, u32[]{:S(2)}) %collective-permute-start.3) | collective-permute-done | bytes 6176 | tf_op jit(solution)/shard_map/ppermute | solution.py:24
  158.8 2.5 %collective-permute-done.5 = f32[2,1,4,128]{3,2,1,0:T(4,128)S(1)} collective-permute-done((f32[2,1,4,128]{3,2,1,0:T(4,128)S(1)}, f32[2,1,4,128]{3,2,1,0:T(4,128)S(1)}, u32[]{:S(2)}, u32[]{:S(2)}) %collective-permute-start.5) | collective-permute-done | bytes 4128 | tf_op jit(solution)/shard_map/ppermute | solution.py:24
  163.5 3.6 %collective-permute-start.7 = (f32[2,6,1,128]{3,2,1,0:T(1,128)S(1)}, f32[2,6,1,128]{3,2,1,0:T(1,128)S(1)}, u32[]{:S(2)}, u32[]{:S(2)}) collective-permute-start(f32[2,6,1,128]{3,2,1,0:T(1,128)S(1)} %get-tuple-element.16), channel_id=1, source_target_pairs={{0,1},{1,2},{2,3},{4,5},{5,6},{6,7},{8,9},{9,10},{10,11},{12,13},{... | collective-permute-start | bytes 18440 | tf_op jit(solution)/shard_map/ppermute | solution.py:24
  167.2 2.8 %collective-permute-done.7 = f32[2,6,1,128]{3,2,1,0:T(1,128)S(1)} collective-permute-done((f32[2,6,1,128]{3,2,1,0:T(1,128)S(1)}, f32[2,6,1,128]{3,2,1,0:T(1,128)S(1)}, u32[]{:S(2)}, u32[]{:S(2)}) %collective-permute-start.7) | collective-permute-done | bytes 6176 | tf_op jit(solution)/shard_map/ppermute | solution.py:24
  174.4 2.5 %collective-permute-done.9 = f32[2,1,4,128]{3,2,1,0:T(4,128)S(1)} collective-permute-done((f32[2,1,4,128]{3,2,1,0:T(4,128)S(1)}, f32[2,1,4,128]{3,2,1,0:T(4,128)S(1)}, u32[]{:S(2)}, u32[]{:S(2)}) %collective-permute-start.9) | collective-permute-done | bytes 4128 | tf_op jit(solution)/shard_map/ppermute | solution.py:24
  178.9 3.9 %collective-permute-start.11 = (f32[2,6,1,128]{3,2,1,0:T(1,128)S(1)}, f32[2,6,1,128]{3,2,1,0:T(1,128)S(1)}, u32[]{:S(2)}, u32[]{:S(2)}) collective-permute-start(f32[2,6,1,128]{3,2,1,0:T(1,128)S(1)} %get-tuple-element.14), channel_id=1, source_target_pairs={{0,1},{1,2},{2,3},{4,5},{5,6},{6,7},{8,9},{9,10},{10,11},{12,13},{... | collective-permute-start | bytes 18440 | tf_op jit(solution)/shard_map/ppermute | solution.py:24
  182.8 2.5 %collective-permute-done.11 = f32[2,6,1,128]{3,2,1,0:T(1,128)S(1)} collective-permute-done((f32[2,6,1,128]{3,2,1,0:T(1,128)S(1)}, f32[2,6,1,128]{3,2,1,0:T(1,128)S(1)}, u32[]{:S(2)}, u32[]{:S(2)}) %collective-permute-start.11) | collective-permute-done | bytes 6176 | tf_op jit(solution)/shard_map/ppermute | solution.py:24
  189.7 2.5 %collective-permute-done.13 = f32[2,1,4,128]{3,2,1,0:T(4,128)S(1)} collective-permute-done((f32[2,1,4,128]{3,2,1,0:T(4,128)S(1)}, f32[2,1,4,128]{3,2,1,0:T(4,128)S(1)}, u32[]{:S(2)}, u32[]{:S(2)}) %collective-permute-start.13) | collective-permute-done | bytes 4128 | tf_op jit(solution)/shard_map/ppermute | solution.py:24
  194.2 3.9 %collective-permute-start.15 = (f32[2,6,1,128]{3,2,1,0:T(1,128)S(1)}, f32[2,6,1,128]{3,2,1,0:T(1,128)S(1)}, u32[]{:S(2)}, u32[]{:S(2)}) collective-permute-start(f32[2,6,1,128]{3,2,1,0:T(1,128)S(1)} %get-tuple-element.12), channel_id=1, source_target_pairs={{0,1},{1,2},{2,3},{4,5},{5,6},{6,7},{8,9},{9,10},{10,11},{12,13},{... | collective-permute-start | bytes 18440 | tf_op jit(solution)/shard_map/ppermute | solution.py:24
  (86 shorter events, 39.3 us)
Async XLA Ops:
  6.5 21.7 %copy-start = (bf16[1,1,32,8,2048]{4,3,2,1,0:T(8,128)(2,1)S(1)}, bf16[1,1,32,8,2048]{4,3,2,1,0:T(8,128)(2,1)}, u32[]{:S(2)}) copy-start(bf16[1,1,32,8,2048]{4,3,2,1,0:T(8,128)(2,1)} %param.9) | copy-start | bytes 3145732
  6.5 81.0 %reduce-scatter.4.cloned.1.call-start = ((), (), s32[]{:S(2)}) async-start(), calls=%async_computation.3 | async-start | bytes 5242880
  23.0 5.2 %copy-start.1 = (bf16[1,1,32,8,2048]{4,3,2,1,0:T(8,128)(2,1)S(1)}, bf16[1,1,32,8,2048]{4,3,2,1,0:T(8,128)(2,1)}, u32[]{:S(2)}) copy-start(bf16[1,1,32,8,2048]{4,3,2,1,0:T(8,128)(2,1)} %param.10) | copy-start | bytes 3145732
  33.7 10.9 %copy-start.4 = (s32[2]{0:T(128)S(1)}, s32[2]{0:T(128)}, u32[]{:S(2)}) copy-start(s32[2]{0:T(128)} %constant.93) | copy-start | bytes 28
  33.7 11.0 %copy-start.5 = (s32[2]{0:T(128)S(1)}, s32[2]{0:T(128)}, u32[]{:S(2)}) copy-start(s32[2]{0:T(128)} %constant.96) | copy-start | bytes 28
  53.4 44.7 %all-to-all-start = ((s32[1,32,128]{2,0,1:T(1,128)}), s32[1,32,128]{2,0,1:T(1,128)S(1)}, u32[]{:S(2)}, u32[]{:S(2)}) async-start(s32[1,32,128]{2,0,1:T(1,128)} %bitcast.7), calls=%async_computation | async-start | bytes 32768 | tf_op jit(solution)/shard_map/all_to_all | solution.py:94
  98.1 10.0 %all-to-all-start.1 = ((f32[2,32,128]{2,0,1:T(2,128)}), f32[2,32,128]{2,0,1:T(2,128)S(1)}, u32[]{:S(2)}, u32[]{:S(2)}) async-start(f32[2,32,128]{2,0,1:T(2,128)} %copy.43), calls=%async_computation.1 | async-start | bytes 65536 | tf_op jit(solution)/shard_map/all_to_all | solution.py:93
  110.2 40.2 %copy-start.2 = (f32[4,4,128]{2,1,0:T(4,128)S(1)}, f32[4,4,128]{2,1,0:T(4,128)}, u32[]{:S(2)}) copy-start(f32[4,4,128]{2,1,0:T(4,128)} %param.15) | copy-start | bytes 24580
  136.6 4.9 %collective-permute-start = (f32[2,1,4,128]{3,2,1,0:T(4,128)S(1)}, f32[2,1,4,128]{3,2,1,0:T(4,128)S(1)}, u32[]{:S(2)}, u32[]{:S(2)}) collective-permute-start(f32[2,1,4,128]{3,2,1,0:T(4,128)S(1)} %get-tuple-element.26), channel_id=1, source_target_pairs={{4,0},{8,4},{12,8},{16,12},{20,16},{24,20},{28,24},{5,1},{9,5},{13... | collective-permute-start | bytes 12296 | tf_op jit(solution)/shard_map/ppermute | solution.py:26
  139.6 4.9 %collective-permute-start.1 = (f32[2,1,4,128]{3,2,1,0:T(4,128)S(1)}, f32[2,1,4,128]{3,2,1,0:T(4,128)S(1)}, u32[]{:S(2)}, u32[]{:S(2)}) collective-permute-start(f32[2,1,4,128]{3,2,1,0:T(4,128)S(1)} %get-tuple-element.25), channel_id=1, source_target_pairs={{0,4},{4,8},{8,12},{12,16},{16,20},{20,24},{24,28},{1,5},{5,9},{9,... | collective-permute-start | bytes 12296 | tf_op jit(solution)/shard_map/ppermute | solution.py:24
  144.5 5.9 %collective-permute-start.2 = (f32[2,6,1,128]{3,2,1,0:T(1,128)S(1)}, f32[2,6,1,128]{3,2,1,0:T(1,128)S(1)}, u32[]{:S(2)}, u32[]{:S(2)}) collective-permute-start(f32[2,6,1,128]{3,2,1,0:T(1,128)S(1)} %get-tuple-element.17), channel_id=1, source_target_pairs={{1,0},{2,1},{3,2},{5,4},{6,5},{7,6},{9,8},{10,9},{11,10},{13,12},{... | collective-permute-start | bytes 18440 | tf_op jit(solution)/shard_map/ppermute | solution.py:26
  147.9 6.4 %collective-permute-start.3 = (f32[2,6,1,128]{3,2,1,0:T(1,128)S(1)}, f32[2,6,1,128]{3,2,1,0:T(1,128)S(1)}, u32[]{:S(2)}, u32[]{:S(2)}) collective-permute-start(f32[2,6,1,128]{3,2,1,0:T(1,128)S(1)} %get-tuple-element.18), channel_id=1, source_target_pairs={{0,1},{1,2},{2,3},{4,5},{5,6},{6,7},{8,9},{9,10},{10,11},{12,13},{... | collective-permute-start | bytes 18440 | tf_op jit(solution)/shard_map/ppermute | solution.py:24
  154.5 4.3 %collective-permute-start.4 = (f32[2,1,4,128]{3,2,1,0:T(4,128)S(1)}, f32[2,1,4,128]{3,2,1,0:T(4,128)S(1)}, u32[]{:S(2)}, u32[]{:S(2)}) collective-permute-start(f32[2,1,4,128]{3,2,1,0:T(4,128)S(1)} %get-tuple-element.24), channel_id=1, source_target_pairs={{4,0},{8,4},{12,8},{16,12},{20,16},{24,20},{28,24},{5,1},{9,5},{13... | collective-permute-start | bytes 12296 | tf_op jit(solution)/shard_map/ppermute | solution.py:26
  156.4 4.9 %collective-permute-start.5 = (f32[2,1,4,128]{3,2,1,0:T(4,128)S(1)}, f32[2,1,4,128]{3,2,1,0:T(4,128)S(1)}, u32[]{:S(2)}, u32[]{:S(2)}) collective-permute-start(f32[2,1,4,128]{3,2,1,0:T(4,128)S(1)} %get-tuple-element.23), channel_id=1, source_target_pairs={{0,4},{4,8},{8,12},{12,16},{16,20},{20,24},{24,28},{1,5},{5,9},{9,... | collective-permute-start | bytes 12296 | tf_op jit(solution)/shard_map/ppermute | solution.py:24
  161.3 5.9 %collective-permute-start.6 = (f32[2,6,1,128]{3,2,1,0:T(1,128)S(1)}, f32[2,6,1,128]{3,2,1,0:T(1,128)S(1)}, u32[]{:S(2)}, u32[]{:S(2)}) collective-permute-start(f32[2,6,1,128]{3,2,1,0:T(1,128)S(1)} %get-tuple-element.15), channel_id=1, source_target_pairs={{1,0},{2,1},{3,2},{5,4},{6,5},{7,6},{9,8},{10,9},{11,10},{13,12},{... | collective-permute-start | bytes 18440 | tf_op jit(solution)/shard_map/ppermute | solution.py:26
  163.5 6.4 %collective-permute-start.7 = (f32[2,6,1,128]{3,2,1,0:T(1,128)S(1)}, f32[2,6,1,128]{3,2,1,0:T(1,128)S(1)}, u32[]{:S(2)}, u32[]{:S(2)}) collective-permute-start(f32[2,6,1,128]{3,2,1,0:T(1,128)S(1)} %get-tuple-element.16), channel_id=1, source_target_pairs={{0,1},{1,2},{2,3},{4,5},{5,6},{6,7},{8,9},{9,10},{10,11},{12,13},{... | collective-permute-start | bytes 18440 | tf_op jit(solution)/shard_map/ppermute | solution.py:24
  170.1 4.3 %collective-permute-start.8 = (f32[2,1,4,128]{3,2,1,0:T(4,128)S(1)}, f32[2,1,4,128]{3,2,1,0:T(4,128)S(1)}, u32[]{:S(2)}, u32[]{:S(2)}) collective-permute-start(f32[2,1,4,128]{3,2,1,0:T(4,128)S(1)} %get-tuple-element.22), channel_id=1, source_target_pairs={{4,0},{8,4},{12,8},{16,12},{20,16},{24,20},{28,24},{5,1},{9,5},{13... | collective-permute-start | bytes 12296 | tf_op jit(solution)/shard_map/ppermute | solution.py:26
  172.0 4.9 %collective-permute-start.9 = (f32[2,1,4,128]{3,2,1,0:T(4,128)S(1)}, f32[2,1,4,128]{3,2,1,0:T(4,128)S(1)}, u32[]{:S(2)}, u32[]{:S(2)}) collective-permute-start(f32[2,1,4,128]{3,2,1,0:T(4,128)S(1)} %get-tuple-element.21), channel_id=1, source_target_pairs={{0,4},{4,8},{8,12},{12,16},{16,20},{20,24},{24,28},{1,5},{5,9},{9,... | collective-permute-start | bytes 12296 | tf_op jit(solution)/shard_map/ppermute | solution.py:24
  176.9 5.9 %collective-permute-start.10 = (f32[2,6,1,128]{3,2,1,0:T(1,128)S(1)}, f32[2,6,1,128]{3,2,1,0:T(1,128)S(1)}, u32[]{:S(2)}, u32[]{:S(2)}) collective-permute-start(f32[2,6,1,128]{3,2,1,0:T(1,128)S(1)} %get-tuple-element.13), channel_id=1, source_target_pairs={{1,0},{2,1},{3,2},{5,4},{6,5},{7,6},{9,8},{10,9},{11,10},{13,12},{... | collective-permute-start | bytes 18440 | tf_op jit(solution)/shard_map/ppermute | solution.py:26
  178.9 6.4 %collective-permute-start.11 = (f32[2,6,1,128]{3,2,1,0:T(1,128)S(1)}, f32[2,6,1,128]{3,2,1,0:T(1,128)S(1)}, u32[]{:S(2)}, u32[]{:S(2)}) collective-permute-start(f32[2,6,1,128]{3,2,1,0:T(1,128)S(1)} %get-tuple-element.14), channel_id=1, source_target_pairs={{0,1},{1,2},{2,3},{4,5},{5,6},{6,7},{8,9},{9,10},{10,11},{12,13},{... | collective-permute-start | bytes 18440 | tf_op jit(solution)/shard_map/ppermute | solution.py:24
  185.4 4.3 %collective-permute-start.12 = (f32[2,1,4,128]{3,2,1,0:T(4,128)S(1)}, f32[2,1,4,128]{3,2,1,0:T(4,128)S(1)}, u32[]{:S(2)}, u32[]{:S(2)}) collective-permute-start(f32[2,1,4,128]{3,2,1,0:T(4,128)S(1)} %get-tuple-element.20), channel_id=1, source_target_pairs={{4,0},{8,4},{12,8},{16,12},{20,16},{24,20},{28,24},{5,1},{9,5},{13... | collective-permute-start | bytes 12296 | tf_op jit(solution)/shard_map/ppermute | solution.py:26
  187.3 4.9 %collective-permute-start.13 = (f32[2,1,4,128]{3,2,1,0:T(4,128)S(1)}, f32[2,1,4,128]{3,2,1,0:T(4,128)S(1)}, u32[]{:S(2)}, u32[]{:S(2)}) collective-permute-start(f32[2,1,4,128]{3,2,1,0:T(4,128)S(1)} %get-tuple-element.19), channel_id=1, source_target_pairs={{0,4},{4,8},{8,12},{12,16},{16,20},{20,24},{24,28},{1,5},{5,9},{9,... | collective-permute-start | bytes 12296 | tf_op jit(solution)/shard_map/ppermute | solution.py:24
  192.3 5.9 %collective-permute-start.14 = (f32[2,6,1,128]{3,2,1,0:T(1,128)S(1)}, f32[2,6,1,128]{3,2,1,0:T(1,128)S(1)}, u32[]{:S(2)}, u32[]{:S(2)}) collective-permute-start(f32[2,6,1,128]{3,2,1,0:T(1,128)S(1)} %get-tuple-element.11), channel_id=1, source_target_pairs={{1,0},{2,1},{3,2},{5,4},{6,5},{7,6},{9,8},{10,9},{11,10},{13,12},{... | collective-permute-start | bytes 18440 | tf_op jit(solution)/shard_map/ppermute | solution.py:26
  194.2 6.4 %collective-permute-start.15 = (f32[2,6,1,128]{3,2,1,0:T(1,128)S(1)}, f32[2,6,1,128]{3,2,1,0:T(1,128)S(1)}, u32[]{:S(2)}, u32[]{:S(2)}) collective-permute-start(f32[2,6,1,128]{3,2,1,0:T(1,128)S(1)} %get-tuple-element.12), channel_id=1, source_target_pairs={{0,1},{1,2},{2,3},{4,5},{5,6},{6,7},{8,9},{9,10},{10,11},{12,13},{... | collective-permute-start | bytes 18440 | tf_op jit(solution)/shard_map/ppermute | solution.py:24
  (2 other events, 5.1 us)
Sparse Core Ops, SparseCore 0:
  33.8 53.6 reduce-scatter.3
where the time goes:
time: 209 us; the launch traced here: 208 us
  waiting for transfers between devices  55.6 us (27%)
  starting transfers between devices  51.9 us (25%)
  other arithmetic  38.9 us (19%)
  local copies, waits for them, and re-layouts  26.9 us (13%)
  blocking collectives  14.4 us (7%)
  between operations  13.8 us (7%)
  matrix products  6.52 us (3%)
    unnamed x2, waiting for transfers between devices  28.3 us
    scatter-add x1, other arithmetic, per_device(): jnp.zeros((NVEC, points + 1), jnp.float32).at[:, received_places[0]]  26 us
    ppermute x8, starting transfers between devices, extended(): lax.ppermute(tail, axis, [(i, (i + 1) % count) for i in range(ends)])  23.1 us
    ppermute x8, waiting for transfers between devices, extended(): lax.ppermute(tail, axis, [(i, (i + 1) % count) for i in range(ends)])  22.2 us
    ppermute x8, starting transfers between devices, extended(): lax.ppermute(head, axis, [((i + 1) % count, i) for i in range(ends)])  18.2 us
    all_gather x1, blocking collectives, per_device(): gathered = lax.all_gather(vectors, 'row', axis=2, tiled=True)  14.4 us
    unnamed x20, local copies, waits for them, and re-layouts  14.2 us
    another operation x2, other arithmetic  9.25 us
  transfers between devices with their start and end apart: 19, of which 10 were waited for; matrix products, arithmetic and copies ran while one was open for 14% of the time, Pallas kernels for 0%

commit v1 on v0

--- a/solution.py
+++ b/solution.py
@@ -90,7 +90,15 @@
     targets = lax.dynamic_slice_in_dim(cluster_perm[0], lax.axis_index("col") * points, points)
     send_values, send_places = route(summed, targets, 1, points, capacity, devices)
     received_values, received_places = (
-        lax.all_to_all(send_values, ("row", "col"), split_axis=1, concat_axis=1, tiled=True),
+        jnp.concatenate(
+            lax.all_to_all(
+                jnp.stack(jnp.split(send_values, lax.axis_size(("row", "col")), axis=1)),
+                ("row", "col"),
+                0,
+                0,
+            ),
+            axis=1,
+        ),
         lax.all_to_all(send_places, ("row", "col"), split_axis=1, concat_axis=1, tiled=True),
     )
     field = (

time: 209 us -> 231 us (1.11)
  local copies, waits for them, and re-layouts: 26.9 us -> 48.4 us
  waiting for transfers between devices: 55.6 us -> 49.2 us
  starting transfers between devices: 51.9 us -> 56.3 us
    unnamed x20 -> x49, local copies, waits for them, and re-layouts: 14.2 us -> 33.5 us
    ppermute x8, waiting for transfers between devices: 22.2 us -> 10.5 us  [extended(): lax.ppermute(tail, axis, [(i, (i + 1) % count) for i in range(ends)])]
    ppermute x8, starting transfers between devices: 18.2 us -> 28.2 us  [extended(): lax.ppermute(head, axis, [((i + 1) % count, i) for i in range(ends)])]
    ppermute x8, starting transfers between devices: 23.1 us -> 17.4 us  [extended(): lax.ppermute(tail, axis, [(i, (i + 1) % count) for i in range(ends)])]
    ppermute x8, waiting for transfers between devices: 0.02 us -> 5.25 us  [extended(): lax.ppermute(head, axis, [((i + 1) % count, i) for i in range(ends)])]
    another operation x5 -> x7, local copies, waits for them, and re-layouts: 0.31 us -> 3.75 us  [the longest x2 3.43 us: per_device(): jnp.stack(jnp.split(send_values, lax.axis_size(('row', 'col')), axis=1))]
    all_to_all x2 -> x0, local copies, waits for them, and re-layouts: 3.21 us -> none  [per_device(): lax.all_to_all(send_values, ('row', 'col'), split_axis=1, concat_axis=1,...]
  transfers between devices with their start and end apart: 19 -> 19, of which waited for: 10 -> 10; matrix products, arithmetic and copies ran while one was open for 14% -> 22% of each run, Pallas kernels for 0% -> 0%
where the time goes in v1:
time: 231 us; the launch traced here: 228 us
  starting transfers between devices  56.3 us (24%)
  waiting for transfers between devices  49.2 us (21%)
  local copies, waits for them, and re-layouts  48.4 us (21%)
  other arithmetic  39.6 us (17%)
  blocking collectives  14.4 us (6%)
  between operations  13.9 us (6%)
  matrix products  6.52 us (3%)
    unnamed x49, local copies, waits for them, and re-layouts  33.5 us
    unnamed x2, waiting for transfers between devices  28.3 us
    ppermute x8, starting transfers between devices, extended(): lax.ppermute(head, axis, [((i + 1) % count, i) for i in range(ends)])  28.2 us
    scatter-add x1, other arithmetic, per_device(): jnp.zeros((NVEC, points + 1), jnp.float32).at[:, received_places[0]]  26 us
    ppermute x8, starting transfers between devices, extended(): lax.ppermute(tail, axis, [(i, (i + 1) % count) for i in range(ends)])  17.4 us
    all_gather x1, blocking collectives, per_device(): gathered = lax.all_gather(vectors, 'row', axis=2, tiled=True)  14.4 us
    ppermute x8, waiting for transfers between devices, extended(): lax.ppermute(tail, axis, [(i, (i + 1) % count) for i in range(ends)])  10.5 us
    another operation x2, other arithmetic  9.25 us
  transfers between devices with their start and end apart: 19, of which 10 were waited for; matrix products, arithmetic and copies ran while one was open for 22% of the time, Pallas kernels for 0%

profile of v1, /device:TPU:12, one launch (start us, length us, event | category | flops | bytes accessed | tf_op | source)
XLA Modules:
  0.0 228.3 jit_solution(12604995572181548420)
XLA Ops:
  8.0 14.4 %all_gather.3 = bf16[2,1,16384]{2,0,1:T(2,128)(2,1)S(1)} all-gather(bf16[2,1,2048]{2,0,1:T(2,128)(2,1)} %param.8), channel_id=1, replica_groups=mesh['row'=8,'col'=4] {'row'}, dimensions={2}, use_global_device_ids=true | all-gather | bytes 73728 | tf_op jit(solution)/shard_map/all_gather | solution.py:60
  25.0 3.5 %fusion.2 = f32[2,8,512]{2,0,1:T(2,128)S(1)} fusion(bf16[1,1,8,512,512]{4,3,2,1,0:T(8,128)(2,1)} %param.12, bf16[8,2,512]{2,1,0:T(2,128)(2,1)S(1)} %gather_fusion, pred[8]{0:T(512)(128)(4,1)S(1)} %and_bitcast_fusion), kind=kOutput, calls=%fused_computation.7 | convolution fusion | flops 8396800 | bytes 4243464 | tf_op jit(solution)/shard_map/lqp,vlp->vlq/dot_general | solution.py:78
  28.9 2.8 %fusion.7 = f32[4,2,2048,1]{2,1,3,0:T(2,128)S(1)} fusion(bf16[4,8,8,2048]{3,2,1,0:T(8,128)(2,1)S(1)} %bitcast.208, bf16[2,8,2048,1]{2,0,1,3:T(2,128)(2,1)S(1)} %bitcast.215, bf16[4,8,8,2048]{3,2,1,0:T(8,128)(2,1)S(1)} %bitcast.212, f32[4,8,8]{2,1,0:T(8,128)S(1)} %fusion.74), kind=kOutput, calls=%fused_computation.11 | convolution fusion | flops 4195328 | bytes 2229248 | tf_op jit(solution)/shard_map/abkp,abvk->vap/dot_general | solution.py:72
  31.7 2.6 %copy.130 = f32[2,8192]{0,1:T(8,128)} copy(f32[2,8192]{1,0:T(2,128)S(1)} %add.151) | data formatting | bytes 131072
  35.2 9.1 %reduce-window.6 = s32[1,32,16,128]{3,2,1,0:T(8,128)S(1)} reduce-window(s32[1,32,16,128]{3,2,1,0:T(8,128)S(1)} %bitcast.211, s32[]{:T(128)} %constant.61.clone.1), window={size=1x1x1x128 pad=0_0x0_0x0_0x127_0}, to_apply=%region_0.1 | reduce-window | flops 8323072 | bytes 524292 | tf_op jit(solution)/shard_map/reduce-window
  45.5 8.6 %scatter_custom_fusion.2 = s32[4096]{0:T(1024)} fusion(s32[2048]{0:T(1024)S(1)} %broadcast_select_fusion.2, s32[2048]{0:T(1024)S(1)} %get-tuple-element.29, s32[]{:T(128)} %constant.60.clone.1), kind=kCustom, calls=%fused_computation.171 | custom fusion | bytes 16388
  54.1 5.8 %all-to-all-start = ((s32[1,32,128]{2,0,1:T(1,128)}), s32[1,32,128]{2,0,1:T(1,128)S(1)}, u32[]{:S(2)}, u32[]{:S(2)}) async-start(s32[1,32,128]{2,0,1:T(1,128)} %bitcast.7), calls=%async_computation | async-start | bytes 32768 | tf_op jit(solution)/shard_map/all_to_all | solution.py:102
  59.9 28.3 %reduce-scatter.4.cloned.1.call-done = f32[2048,2]{1,0:T(8,128)} async-done(((f32[8192,2]{1,0:T(8,128)}), f32[2048,2]{1,0:T(8,128)}) %reduce-scatter.4.cloned.1.call-update) | async-done | bytes 16400
  91.1 6.5 %scatter_custom_fusion = f32[2,4096]{0,1:T(8,128)S(1)} fusion(s32[2048]{0:T(1024)S(1)} %bitcast.219, f32[2048,2]{1,0:T(8,128)} %copy.119, f32[]{:T(128)} %constant.59.clone.1), kind=kCustom, calls=%fused_computation.12 | custom fusion | bytes 33280 | tf_op jit(solution)/shard_map/scatter | solution.py:52
  117.5 2.8 %copy.120 = f32[32,2,128]{2,1,0:T(2,128)} copy(f32[32,2,128]{1,2,0:T(8,128)} %fusion.13) | data formatting | bytes 65536 | tf_op jit(solution)/shard_map/stack | solution.py:95
  120.3 4.9 %all-to-all-start.1 = ((f32[32,2,128]{2,1,0:T(2,128)}), f32[32,2,128]{2,1,0:T(2,128)S(1)}, u32[]{:S(2)}, u32[]{:S(2)}) async-start(f32[32,2,128]{2,1,0:T(2,128)} %copy.120), calls=%async_computation.1 | async-start | bytes 65536 | tf_op jit(solution)/shard_map/all_to_all | solution.py:94
  125.2 5.1 %all-to-all-done.1 = f32[32,2,128]{2,1,0:T(2,128)S(1)} async-done(((f32[32,2,128]{2,1,0:T(2,128)}), f32[32,2,128]{2,1,0:T(2,128)S(1)}, u32[]{:S(2)}, u32[]{:S(2)}) %all-to-all-start.1) | async-done | bytes 32800 | tf_op jit(solution)/shard_map/all_to_all | solution.py:94
  132.3 26.0 %scatter_custom_fusion.1 = f32[2,2049]{0,1:T(8,128)S(1)} fusion(s32[4096]{0:T(1024)S(1)} %bitcast.224, f32[4096,2]{1,0:T(8,128)} %copy.121, f32[]{:T(128)} %constant.59.clone.1), kind=kCustom, calls=%fused_computation.14 | custom fusion | flops 8192 | bytes 16904 | tf_op jit(solution)/shard_map/scatter-add | solution.py:105
  158.8 3.0 %collective-permute-start = (f32[2,1,4,128]{3,2,1,0:T(4,128)S(1)}, f32[2,1,4,128]{3,2,1,0:T(4,128)S(1)}, u32[]{:S(2)}, u32[]{:S(2)}) collective-permute-start(f32[2,1,4,128]{3,2,1,0:T(4,128)S(1)} %get-tuple-element.26), channel_id=1, source_target_pairs={{4,0},{8,4},{12,8},{16,12},{20,16},{24,20},{28,24},{5,1},{9,5},{13... | collective-permute-start | bytes 12296 | tf_op jit(solution)/shard_map/ppermute | solution.py:26
  163.7 3.0 %collective-permute-done.1 = f32[2,1,4,128]{3,2,1,0:T(4,128)S(1)} collective-permute-done((f32[2,1,4,128]{3,2,1,0:T(4,128)S(1)}, f32[2,1,4,128]{3,2,1,0:T(4,128)S(1)}, u32[]{:S(2)}, u32[]{:S(2)}) %collective-permute-start.1) | collective-permute-done | bytes 4128 | tf_op jit(solution)/shard_map/ppermute | solution.py:24
  166.7 2.5 %collective-permute-start.3 = (f32[2,6,1,128]{3,2,1,0:T(1,128)S(1)}, f32[2,6,1,128]{3,2,1,0:T(1,128)S(1)}, u32[]{:S(2)}, u32[]{:S(2)}) collective-permute-start(f32[2,6,1,128]{3,2,1,0:T(1,128)S(1)} %get-tuple-element.18), channel_id=1, source_target_pairs={{0,1},{1,2},{2,3},{4,5},{5,6},{6,7},{8,9},{9,10},{10,11},{12,13},{... | collective-permute-start | bytes 18440 | tf_op jit(solution)/shard_map/ppermute | solution.py:24
  169.2 4.2 %collective-permute-start.2 = (f32[2,6,1,128]{3,2,1,0:T(1,128)S(1)}, f32[2,6,1,128]{3,2,1,0:T(1,128)S(1)}, u32[]{:S(2)}, u32[]{:S(2)}) collective-permute-start(f32[2,6,1,128]{3,2,1,0:T(1,128)S(1)} %get-tuple-element.17), channel_id=1, source_target_pairs={{1,0},{2,1},{3,2},{5,4},{6,5},{7,6},{9,8},{10,9},{11,10},{13,12},{... | collective-permute-start | bytes 18440 | tf_op jit(solution)/shard_map/ppermute | solution.py:26
  176.8 2.4 %collective-permute-start.5 = (f32[2,1,4,128]{3,2,1,0:T(4,128)S(1)}, f32[2,1,4,128]{3,2,1,0:T(4,128)S(1)}, u32[]{:S(2)}, u32[]{:S(2)}) collective-permute-start(f32[2,1,4,128]{3,2,1,0:T(4,128)S(1)} %get-tuple-element.23), channel_id=1, source_target_pairs={{0,4},{4,8},{8,12},{12,16},{16,20},{20,24},{24,28},{1,5},{5,9},{9,... | collective-permute-start | bytes 12296 | tf_op jit(solution)/shard_map/ppermute | solution.py:24
  179.2 2.5 %collective-permute-done.5 = f32[2,1,4,128]{3,2,1,0:T(4,128)S(1)} collective-permute-done((f32[2,1,4,128]{3,2,1,0:T(4,128)S(1)}, f32[2,1,4,128]{3,2,1,0:T(4,128)S(1)}, u32[]{:S(2)}, u32[]{:S(2)}) %collective-permute-start.5) | collective-permute-done | bytes 4128 | tf_op jit(solution)/shard_map/ppermute | solution.py:24
  183.7 5.1 %collective-permute-start.6 = (f32[2,6,1,128]{3,2,1,0:T(1,128)S(1)}, f32[2,6,1,128]{3,2,1,0:T(1,128)S(1)}, u32[]{:S(2)}, u32[]{:S(2)}) collective-permute-start(f32[2,6,1,128]{3,2,1,0:T(1,128)S(1)} %get-tuple-element.15), channel_id=1, source_target_pairs={{1,0},{2,1},{3,2},{5,4},{6,5},{7,6},{9,8},{10,9},{11,10},{13,12},{... | collective-permute-start | bytes 18440 | tf_op jit(solution)/shard_map/ppermute | solution.py:26
  194.6 2.5 %collective-permute-done.9 = f32[2,1,4,128]{3,2,1,0:T(4,128)S(1)} collective-permute-done((f32[2,1,4,128]{3,2,1,0:T(4,128)S(1)}, f32[2,1,4,128]{3,2,1,0:T(4,128)S(1)}, u32[]{:S(2)}, u32[]{:S(2)}) %collective-permute-start.9) | collective-permute-done | bytes 4128 | tf_op jit(solution)/shard_map/ppermute | solution.py:24
  199.0 5.1 %collective-permute-start.10 = (f32[2,6,1,128]{3,2,1,0:T(1,128)S(1)}, f32[2,6,1,128]{3,2,1,0:T(1,128)S(1)}, u32[]{:S(2)}, u32[]{:S(2)}) collective-permute-start(f32[2,6,1,128]{3,2,1,0:T(1,128)S(1)} %get-tuple-element.13), channel_id=1, source_target_pairs={{1,0},{2,1},{3,2},{5,4},{6,5},{7,6},{9,8},{10,9},{11,10},{13,12},{... | collective-permute-start | bytes 18440 | tf_op jit(solution)/shard_map/ppermute | solution.py:26
  209.9 2.5 %collective-permute-done.13 = f32[2,1,4,128]{3,2,1,0:T(4,128)S(1)} collective-permute-done((f32[2,1,4,128]{3,2,1,0:T(4,128)S(1)}, f32[2,1,4,128]{3,2,1,0:T(4,128)S(1)}, u32[]{:S(2)}, u32[]{:S(2)}) %collective-permute-start.13) | collective-permute-done | bytes 4128 | tf_op jit(solution)/shard_map/ppermute | solution.py:24
  214.3 5.1 %collective-permute-start.14 = (f32[2,6,1,128]{3,2,1,0:T(1,128)S(1)}, f32[2,6,1,128]{3,2,1,0:T(1,128)S(1)}, u32[]{:S(2)}, u32[]{:S(2)}) collective-permute-start(f32[2,6,1,128]{3,2,1,0:T(1,128)S(1)} %get-tuple-element.11), channel_id=1, source_target_pairs={{1,0},{2,1},{3,2},{5,4},{6,5},{7,6},{9,8},{10,9},{11,10},{13,12},{... | collective-permute-start | bytes 18440 | tf_op jit(solution)/shard_map/ppermute | solution.py:26
  (116 shorter events, 56.2 us)
Async XLA Ops:
  6.5 22.3 %copy-start = (bf16[1,1,32,8,2048]{4,3,2,1,0:T(8,128)(2,1)S(1)}, bf16[1,1,32,8,2048]{4,3,2,1,0:T(8,128)(2,1)}, u32[]{:S(2)}) copy-start(bf16[1,1,32,8,2048]{4,3,2,1,0:T(8,128)(2,1)} %param.9) | copy-start | bytes 3145732
  6.5 81.6 %reduce-scatter.4.cloned.1.call-start = ((), (), s32[]{:S(2)}) async-start(), calls=%async_computation.3 | async-start | bytes 5242880
  25.0 3.9 %copy-start.1 = (bf16[1,1,32,8,2048]{4,3,2,1,0:T(8,128)(2,1)S(1)}, bf16[1,1,32,8,2048]{4,3,2,1,0:T(8,128)(2,1)}, u32[]{:S(2)}) copy-start(bf16[1,1,32,8,2048]{4,3,2,1,0:T(8,128)(2,1)} %param.10) | copy-start | bytes 3145732
  34.3 10.9 %copy-start.5 = (s32[2]{0:T(128)S(1)}, s32[2]{0:T(128)}, u32[]{:S(2)}) copy-start(s32[2]{0:T(128)} %constant.96) | copy-start | bytes 28
  34.3 11.0 %copy-start.4 = (s32[2]{0:T(128)S(1)}, s32[2]{0:T(128)}, u32[]{:S(2)}) copy-start(s32[2]{0:T(128)} %constant.93) | copy-start | bytes 28
  54.1 66.2 %all-to-all-start = ((s32[1,32,128]{2,0,1:T(1,128)}), s32[1,32,128]{2,0,1:T(1,128)S(1)}, u32[]{:S(2)}, u32[]{:S(2)}) async-start(s32[1,32,128]{2,0,1:T(1,128)} %bitcast.7), calls=%async_computation | async-start | bytes 32768 | tf_op jit(solution)/shard_map/all_to_all | solution.py:102
  120.3 10.0 %all-to-all-start.1 = ((f32[32,2,128]{2,1,0:T(2,128)}), f32[32,2,128]{2,1,0:T(2,128)S(1)}, u32[]{:S(2)}, u32[]{:S(2)}) async-start(f32[32,2,128]{2,1,0:T(2,128)} %copy.120), calls=%async_computation.1 | async-start | bytes 65536 | tf_op jit(solution)/shard_map/all_to_all | solution.py:94
  132.3 41.1 %copy-start.2 = (f32[4,4,128]{2,1,0:T(4,128)S(1)}, f32[4,4,128]{2,1,0:T(4,128)}, u32[]{:S(2)}) copy-start(f32[4,4,128]{2,1,0:T(4,128)} %param.15) | copy-start | bytes 24580
  158.8 4.9 %collective-permute-start = (f32[2,1,4,128]{3,2,1,0:T(4,128)S(1)}, f32[2,1,4,128]{3,2,1,0:T(4,128)S(1)}, u32[]{:S(2)}, u32[]{:S(2)}) collective-permute-start(f32[2,1,4,128]{3,2,1,0:T(4,128)S(1)} %get-tuple-element.26), channel_id=1, source_target_pairs={{4,0},{8,4},{12,8},{16,12},{20,16},{24,20},{28,24},{5,1},{9,5},{13... | collective-permute-start | bytes 12296 | tf_op jit(solution)/shard_map/ppermute | solution.py:26
  161.8 4.9 %collective-permute-start.1 = (f32[2,1,4,128]{3,2,1,0:T(4,128)S(1)}, f32[2,1,4,128]{3,2,1,0:T(4,128)S(1)}, u32[]{:S(2)}, u32[]{:S(2)}) collective-permute-start(f32[2,1,4,128]{3,2,1,0:T(4,128)S(1)} %get-tuple-element.25), channel_id=1, source_target_pairs={{0,4},{4,8},{8,12},{12,16},{16,20},{20,24},{24,28},{1,5},{5,9},{9,... | collective-permute-start | bytes 12296 | tf_op jit(solution)/shard_map/ppermute | solution.py:24
  166.7 6.8 %collective-permute-start.3 = (f32[2,6,1,128]{3,2,1,0:T(1,128)S(1)}, f32[2,6,1,128]{3,2,1,0:T(1,128)S(1)}, u32[]{:S(2)}, u32[]{:S(2)}) collective-permute-start(f32[2,6,1,128]{3,2,1,0:T(1,128)S(1)} %get-tuple-element.18), channel_id=1, source_target_pairs={{0,1},{1,2},{2,3},{4,5},{5,6},{6,7},{8,9},{9,10},{10,11},{12,13},{... | collective-permute-start | bytes 18440 | tf_op jit(solution)/shard_map/ppermute | solution.py:24
  169.2 5.6 %collective-permute-start.2 = (f32[2,6,1,128]{3,2,1,0:T(1,128)S(1)}, f32[2,6,1,128]{3,2,1,0:T(1,128)S(1)}, u32[]{:S(2)}, u32[]{:S(2)}) collective-permute-start(f32[2,6,1,128]{3,2,1,0:T(1,128)S(1)} %get-tuple-element.17), channel_id=1, source_target_pairs={{1,0},{2,1},{3,2},{5,4},{6,5},{7,6},{9,8},{10,9},{11,10},{13,12},{... | collective-permute-start | bytes 18440 | tf_op jit(solution)/shard_map/ppermute | solution.py:26
  174.9 4.3 %collective-permute-start.4 = (f32[2,1,4,128]{3,2,1,0:T(4,128)S(1)}, f32[2,1,4,128]{3,2,1,0:T(4,128)S(1)}, u32[]{:S(2)}, u32[]{:S(2)}) collective-permute-start(f32[2,1,4,128]{3,2,1,0:T(4,128)S(1)} %get-tuple-element.24), channel_id=1, source_target_pairs={{4,0},{8,4},{12,8},{16,12},{20,16},{24,20},{28,24},{5,1},{9,5},{13... | collective-permute-start | bytes 12296 | tf_op jit(solution)/shard_map/ppermute | solution.py:26
  176.8 4.9 %collective-permute-start.5 = (f32[2,1,4,128]{3,2,1,0:T(4,128)S(1)}, f32[2,1,4,128]{3,2,1,0:T(4,128)S(1)}, u32[]{:S(2)}, u32[]{:S(2)}) collective-permute-start(f32[2,1,4,128]{3,2,1,0:T(4,128)S(1)} %get-tuple-element.23), channel_id=1, source_target_pairs={{0,4},{4,8},{8,12},{12,16},{16,20},{20,24},{24,28},{1,5},{5,9},{9,... | collective-permute-start | bytes 12296 | tf_op jit(solution)/shard_map/ppermute | solution.py:24
  181.8 7.0 %collective-permute-start.7 = (f32[2,6,1,128]{3,2,1,0:T(1,128)S(1)}, f32[2,6,1,128]{3,2,1,0:T(1,128)S(1)}, u32[]{:S(2)}, u32[]{:S(2)}) collective-permute-start(f32[2,6,1,128]{3,2,1,0:T(1,128)S(1)} %get-tuple-element.16), channel_id=1, source_target_pairs={{0,1},{1,2},{2,3},{4,5},{5,6},{6,7},{8,9},{9,10},{10,11},{12,13},{... | collective-permute-start | bytes 18440 | tf_op jit(solution)/shard_map/ppermute | solution.py:24
  183.7 6.4 %collective-permute-start.6 = (f32[2,6,1,128]{3,2,1,0:T(1,128)S(1)}, f32[2,6,1,128]{3,2,1,0:T(1,128)S(1)}, u32[]{:S(2)}, u32[]{:S(2)}) collective-permute-start(f32[2,6,1,128]{3,2,1,0:T(1,128)S(1)} %get-tuple-element.15), channel_id=1, source_target_pairs={{1,0},{2,1},{3,2},{5,4},{6,5},{7,6},{9,8},{10,9},{11,10},{13,12},{... | collective-permute-start | bytes 18440 | tf_op jit(solution)/shard_map/ppermute | solution.py:26
  190.2 4.3 %collective-permute-start.8 = (f32[2,1,4,128]{3,2,1,0:T(4,128)S(1)}, f32[2,1,4,128]{3,2,1,0:T(4,128)S(1)}, u32[]{:S(2)}, u32[]{:S(2)}) collective-permute-start(f32[2,1,4,128]{3,2,1,0:T(4,128)S(1)} %get-tuple-element.22), channel_id=1, source_target_pairs={{4,0},{8,4},{12,8},{16,12},{20,16},{24,20},{28,24},{5,1},{9,5},{13... | collective-permute-start | bytes 12296 | tf_op jit(solution)/shard_map/ppermute | solution.py:26
  192.1 4.9 %collective-permute-start.9 = (f32[2,1,4,128]{3,2,1,0:T(4,128)S(1)}, f32[2,1,4,128]{3,2,1,0:T(4,128)S(1)}, u32[]{:S(2)}, u32[]{:S(2)}) collective-permute-start(f32[2,1,4,128]{3,2,1,0:T(4,128)S(1)} %get-tuple-element.21), channel_id=1, source_target_pairs={{0,4},{4,8},{8,12},{12,16},{16,20},{20,24},{24,28},{1,5},{5,9},{9,... | collective-permute-start | bytes 12296 | tf_op jit(solution)/shard_map/ppermute | solution.py:24
  197.1 7.0 %collective-permute-start.11 = (f32[2,6,1,128]{3,2,1,0:T(1,128)S(1)}, f32[2,6,1,128]{3,2,1,0:T(1,128)S(1)}, u32[]{:S(2)}, u32[]{:S(2)}) collective-permute-start(f32[2,6,1,128]{3,2,1,0:T(1,128)S(1)} %get-tuple-element.14), channel_id=1, source_target_pairs={{0,1},{1,2},{2,3},{4,5},{5,6},{6,7},{8,9},{9,10},{10,11},{12,13},{... | collective-permute-start | bytes 18440 | tf_op jit(solution)/shard_map/ppermute | solution.py:24
  199.0 6.4 %collective-permute-start.10 = (f32[2,6,1,128]{3,2,1,0:T(1,128)S(1)}, f32[2,6,1,128]{3,2,1,0:T(1,128)S(1)}, u32[]{:S(2)}, u32[]{:S(2)}) collective-permute-start(f32[2,6,1,128]{3,2,1,0:T(1,128)S(1)} %get-tuple-element.13), channel_id=1, source_target_pairs={{1,0},{2,1},{3,2},{5,4},{6,5},{7,6},{9,8},{10,9},{11,10},{13,12},{... | collective-permute-start | bytes 18440 | tf_op jit(solution)/shard_map/ppermute | solution.py:26
  205.5 4.3 %collective-permute-start.12 = (f32[2,1,4,128]{3,2,1,0:T(4,128)S(1)}, f32[2,1,4,128]{3,2,1,0:T(4,128)S(1)}, u32[]{:S(2)}, u32[]{:S(2)}) collective-permute-start(f32[2,1,4,128]{3,2,1,0:T(4,128)S(1)} %get-tuple-element.20), channel_id=1, source_target_pairs={{4,0},{8,4},{12,8},{16,12},{20,16},{24,20},{28,24},{5,1},{9,5},{13... | collective-permute-start | bytes 12296 | tf_op jit(solution)/shard_map/ppermute | solution.py:26
  207.4 4.9 %collective-permute-start.13 = (f32[2,1,4,128]{3,2,1,0:T(4,128)S(1)}, f32[2,1,4,128]{3,2,1,0:T(4,128)S(1)}, u32[]{:S(2)}, u32[]{:S(2)}) collective-permute-start(f32[2,1,4,128]{3,2,1,0:T(4,128)S(1)} %get-tuple-element.19), channel_id=1, source_target_pairs={{0,4},{4,8},{8,12},{12,16},{16,20},{20,24},{24,28},{1,5},{5,9},{9,... | collective-permute-start | bytes 12296 | tf_op jit(solution)/shard_map/ppermute | solution.py:24
  212.4 7.0 %collective-permute-start.15 = (f32[2,6,1,128]{3,2,1,0:T(1,128)S(1)}, f32[2,6,1,128]{3,2,1,0:T(1,128)S(1)}, u32[]{:S(2)}, u32[]{:S(2)}) collective-permute-start(f32[2,6,1,128]{3,2,1,0:T(1,128)S(1)} %get-tuple-element.12), channel_id=1, source_target_pairs={{0,1},{1,2},{2,3},{4,5},{5,6},{6,7},{8,9},{9,10},{10,11},{12,13},{... | collective-permute-start | bytes 18440 | tf_op jit(solution)/shard_map/ppermute | solution.py:24
  214.3 6.4 %collective-permute-start.14 = (f32[2,6,1,128]{3,2,1,0:T(1,128)S(1)}, f32[2,6,1,128]{3,2,1,0:T(1,128)S(1)}, u32[]{:S(2)}, u32[]{:S(2)}) collective-permute-start(f32[2,6,1,128]{3,2,1,0:T(1,128)S(1)} %get-tuple-element.11), channel_id=1, source_target_pairs={{1,0},{2,1},{3,2},{5,4},{6,5},{7,6},{9,8},{10,9},{11,10},{13,12},{... | collective-permute-start | bytes 18440 | tf_op jit(solution)/shard_map/ppermute | solution.py:26
  (1 other events, 0.8 us)
Sparse Core Ops, SparseCore 0:
  34.5 53.6 reduce-scatter.3
